TPU v7x, 256 devices: a whole 4x4x8 slice. The times are simulated.
256 devices in a mesh: grp: 2 (over z_hi), dev: 128 (over x, z_lo, y, core).
Axes of the slice: x: 4, y: 4, z: 8 (z_hi: 2, z_lo: 4; z = z_hi * 4 + z_lo), core: 2. Of those that a mesh axis runs over, the one named last changes fastest.
Arguments:
- voltages: int32 [512, 137216], P('dev', 'grp'), may hold values from -2147483648 to 2147483646
- block_order: int32 [10], replicated, may hold values from 0 to 9, each once
Outputs:
- visibilities: float32 [10, 2, 2, 1024, 128, 128], P('grp', None, None, 'dev')
Inputs may be any that keep to these rules, and one draw needn't show every extreme that they name: `block_order`: a permutation of the block pair numbers.
All inputs are finite; a program needn't handle non-finite values.
Results may differ from a plain program's by a relative error of at most 0.0058.
Values may be sent and summed in bfloat16 or wider, within the bound.
A program may use at most 128 MiB of HBM per device.

v0:
```python
import jax
import jax.numpy as jnp
import numpy as np
from jax import lax
from jax.sharding import PartitionSpec as P

A = 512
FREQ_CHANNELS = 1024
FILTER_TAPS = 4
BLOCK_FRAMES = 64
INTEG_PERIODS = 2
BLOCK = 128


def unpack_packed_words(words):
    pieces = []
    for byte in range(4):
        raw = jnp.bitwise_and(jnp.right_shift(words, 8 * byte), 255)
        pieces.append((raw - 128).astype(jnp.float32) / 64.0)
    return jnp.concatenate(pieces, axis=-1)


def prototype():
    length = 2 * FREQ_CHANNELS
    position = jnp.arange(FILTER_TAPS * length, dtype=jnp.float32) + 0.5
    window = 0.5 - 0.5 * jnp.cos(2.0 * jnp.pi * position / (length * FILTER_TAPS))
    return jnp.sinc(position / length - FILTER_TAPS / 2.0) * window


def dft_table():
    length = 2 * FREQ_CHANNELS
    index = (
        jnp.arange(length, dtype=jnp.int32)[:, None]
        * jnp.arange(FREQ_CHANNELS, dtype=jnp.int32)[None, :]
    )
    angle = 2.0 * jnp.pi / length * (index % length).astype(jnp.float32)
    factor = length ** (-0.5)
    return jnp.stack([jnp.cos(angle) * factor, -jnp.sin(angle) * factor], axis=1).astype(
        jnp.bfloat16
    )


def filter_frames(voltage_samples, coeffs):
    weights = coeffs.reshape(FILTER_TAPS, 2 * FREQ_CHANNELS)
    total = voltage_samples[..., 0:BLOCK_FRAMES, :] * weights[0]
    for shift in range(1, FILTER_TAPS):
        total = total + voltage_samples[..., shift : shift + BLOCK_FRAMES, :] * weights[shift]
    return total.astype(jnp.bfloat16)


def pick(table, index):
    hits = jnp.arange(table.shape[0], dtype=jnp.int32) == index
    return jnp.sum(jnp.where(hits, table, 0)).astype(jnp.int32)


def twist_parts(data):
    width = data.shape[3]
    split = data.reshape(data.shape[:3] + (width // (2 * BLOCK_FRAMES), 2, BLOCK_FRAMES))
    return jnp.stack([split[..., 1, :], -split[..., 0, :]], axis=-2).reshape(data.shape)


def block_gram(data, twisted, slots, block_order, factor):
    upper_rows, upper_cols = np.triu_indices(A // BLOCK)
    pair_rows = jnp.asarray(upper_rows.astype(np.int32))
    pair_cols = jnp.asarray(upper_cols.astype(np.int32))

    def one_slot(slot):
        entry = pick(block_order, slot)
        row = pick(pair_rows, entry) * BLOCK
        col = pick(pair_cols, entry) * BLOCK
        left = lax.dynamic_slice_in_dim(data, row, BLOCK, 2)
        left_twist = lax.dynamic_slice_in_dim(twisted, row, BLOCK, 2)
        right = lax.dynamic_slice_in_dim(data, col, BLOCK, 2)
        real = jnp.einsum("ciak,cibk->icab", left, right, preferred_element_type=jnp.float32)
        imag = jnp.einsum("ciak,cibk->icab", left_twist, right, preferred_element_type=jnp.float32)
        return jnp.stack([real, imag], axis=1) * factor

    return lax.map(one_slot, slots)


def on_device(voltages, block_order):
    antennas_per_device = voltages.shape[0]
    groups = lax.axis_size("grp")
    factor = 1.0 / (groups * BLOCK_FRAMES)
    pair_count = A // BLOCK * (A // BLOCK + 1) // 2
    owned_count = pair_count // groups
    coeffs = prototype()
    table = dft_table()
    voltage_samples = unpack_packed_words(
        voltages.reshape(antennas_per_device, INTEG_PERIODS, -1)
    ).reshape(antennas_per_device, INTEG_PERIODS, BLOCK_FRAMES + FILTER_TAPS - 1, 2 * FREQ_CHANNELS)
    filtered = filter_frames(voltage_samples, coeffs)
    channel_spectra = jnp.einsum(
        "aifn,nrc->ciarf", filtered, table, preferred_element_type=jnp.float32
    )
    channel_spectra = channel_spectra.astype(jnp.bfloat16).reshape(
        FREQ_CHANNELS, INTEG_PERIODS, antennas_per_device, 2 * BLOCK_FRAMES
    )
    data = lax.all_to_all(channel_spectra, "dev", split_axis=0, concat_axis=2, tiled=True)
    twisted = twist_parts(data)
    owned = lax.axis_index("grp") * owned_count + jnp.arange(owned_count, dtype=jnp.int32)
    return block_gram(
        lax.all_gather(data, "grp", axis=3, tiled=True),
        lax.all_gather(twisted, "grp", axis=3, tiled=True),
        owned,
        block_order,
        factor,
    )


def solution(mesh):
    in_specs = (P("dev", "grp"), P())
    out_specs = P("grp", None, None, "dev", None, None)
    return jax.shard_map(
        on_device, mesh=mesh, in_specs=in_specs, out_specs=out_specs, check_vma=False
    )
```

profile of v0, /device:TPU:1, one launch (start us, length us, event | category | flops | bytes accessed | tf_op | source)
XLA Modules:
  0.0 431.1 jit_solution(8316655637687082720)
XLA Ops:
  6.7 35.2 %multiply_convert_fusion = (bf16[2048,1,1024]{2,0,1:T(8,128)(2,1)}, bf16[2048,1,1024]{2,0,1:T(8,128)(2,1)}) fusion(), kind=kLoop, calls=%fused_computation.27 | loop fusion | flops 39845888 | bytes 8388608 | tf_op jit(solution)/shard_map/convert.1
  41.9 2.7 convert_multiply_fusion.3
  46.9 2.4 reshape.173
  49.2 3.4 reshape.175
  52.7 10.2 %pad_maximum_fusion = f32[4,2,137216]{2,1,0:T(2,128)} fusion(f32[4,2,34304]{2,1,0:T(2,128)} %reshape.175, f32[4,2,34304]{2,1,0:T(2,128)S(1)} %reshape.173, f32[4,2,34304]{2,1,0:T(2,128)S(1)} %reshape.171, f32[4,2,34304]{2,1,0:T(2,128)S(1)} %reshape.169), kind=kLoop, calls=%fused_computation.32 | loop fusion | flops 3293184 | bytes 8781824 | tf_op jit(solution)/shard_map/concatenate | solution.py:20
  62.8 6.9 %reshape.164 = f32[4,2,67,2048]{3,2,1,0:T(8,128)} reshape(f32[4,2,137216]{2,1,0:T(2,128)} %pad_maximum_fusion) | data formatting | bytes 8781824 | tf_op jit(solution)/shard_map/reshape | solution.py:91
  69.7 14.4 %convert_bitcast_fusion = bf16[1024,2,4,2,64]{0,4,1,2,3:T(8,128)(2,1)S(1)} fusion(f32[2048]{0:T(1024)S(1)} %get-tuple-element.110, f32[4,2,67,2048]{3,2,1,0:T(8,128)} %reshape.164, f32[2048]{0:T(1024)S(1)} %get-tuple-element.111, f32[2048]{0:T(1024)S(1)} %get-tuple-element.112, f32[2048]{0:T(1024)S(1)} %get-tuple-element.109, ...), kind=kOutput, calls=%fused_computation.45 | convolution fusion | flops 4321181696 | bytes 27295744 | tf_op jit(solution)/shard_map/aifn,nrc->ciarf/dot_general | solution.py:93
  84.3 2.7 copy.21
  87.0 65.7 %all_to_all.18 = bf16[1024,2,4,128]{3,2,1,0:T(4,128)(2,1)S(1)} all-to-all(bf16[1024,2,4,128]{3,2,1,0:T(4,128)(2,1)} %copy.21), channel_id=1, replica_groups=mesh['grp'=2,'dev'=128] {'dev'}, dimensions={0} | all-to-all | bytes 4194304 | tf_op jit(solution)/shard_map/all_to_all | solution.py:99
  153.0 1.7 copy.23
  154.7 8.4 %reshape.166 = bf16[8,2,512,1,2,64]{5,4,0,2,1,3:T(2,128)(2,1)} reshape(bf16[8,2,128,4,128]{4,0,3,2,1:T(8,128)(2,1)} %copy.23) | data formatting | bytes 4194304 | tf_op jit(solution)/shard_map/reshape | solution.py:58
  163.2 9.6 %fusion.43 = (bf16[8,2,512,1,1,64]{5,4,0,2,1,3:T(2,128)(2,1)S(1)}, bf16[8,2,512,1,1,64]{5,4,0,2,1,3:T(2,128)(2,1)S(1)}) fusion(bf16[8,2,512,1,2,64]{5,4,0,2,1,3:T(2,128)(2,1)} %reshape.166), kind=kLoop, calls=%fused_computation.79 | loop fusion | flops 524288 | bytes 4194304 | tf_op jit(solution)/shard_map/slice | solution.py:59
  172.8 12.0 %pad_maximum_fusion.1 = bf16[8,2,512,1,2,64]{5,4,0,2,1,3:T(2,128)(2,1)} fusion(bf16[8,2,512,1,1,64]{5,4,0,2,1,3:T(2,128)(2,1)S(1)} %get-tuple-element.104, bf16[8,2,512,1,1,64]{5,4,0,2,1,3:T(2,128)(2,1)S(1)} %get-tuple-element.103), kind=kLoop, calls=%fused_computation.42 | loop fusion | flops 4194304 | bytes 4194304 | tf_op jit(solution)/shard_map/stack | solution.py:59
  184.9 10.6 %copy.25 = bf16[8,2,512,1,2,64]{2,5,4,1,0,3:T(8,128)(2,1)} copy(bf16[8,2,512,1,2,64]{5,4,0,2,1,3:T(2,128)(2,1)} %pad_maximum_fusion.1) | data formatting | bytes 4194304 | tf_op jit(solution)/shard_map/stack | solution.py:59
  195.5 68.0 %all-gather.3.cloned.1.call-done = bf16[8,2,512,256]{3,0,2,1:T(8,128)(2,1)} async-done(((bf16[8,2,512,128]{3,0,2,1:T(8,128)(2,1)}), bf16[8,2,512,256]{3,0,2,1:T(8,128)(2,1)}) %all-gather.3.cloned.1.call-update) | async-done | bytes 4194320 | tf_op jit(solution)/shard_map/all_gather | solution.py:103
  263.5 5.1 %copy.26 = bf16[8,2,512,256]{3,2,0,1:T(8,128)(2,1)} copy(bf16[8,2,512,256]{3,0,2,1:T(8,128)(2,1)} %all-gather.3.cloned.1.call-done) | data formatting | bytes 8388608
  268.6 104.8 %all-gather.5.cloned.1.call-done = bf16[8,2,512,256]{2,3,1,0:T(8,128)(2,1)} async-done(((bf16[8,2,512,128]{2,3,1,0:T(8,128)(2,1)}), bf16[8,2,512,256]{2,3,1,0:T(8,128)(2,1)}) %all-gather.5.cloned.1.call-update) | async-done | bytes 4194320 | tf_op jit(solution)/shard_map/all_gather | solution.py:104
  373.4 50.9 %while.11 = (s32[]{:T(128)}, f32[5,2,2,8,128,128]{5,4,3,2,1,0:T(8,128)}, s32[5]{0:T(128)S(1)}, s32[10]{0:T(128)S(1)}, bf16[8,2,512,256]{3,2,0,1:T(8,128)(2,1)}, ...) while((s32[]{:T(128)}, ...), condition=%wide.region_4.5_spmd.clone, body=%wide.region_0.4_spmd.sunk.clone.sunk | while | flops 269484096 | bytes 10486649 | solution.py:78
  378.0 2.0 convolution_bitcast_fusion.5
  380.0 2.0 convolution_bitcast_fusion.4
  382.1 1.5 copy_dynamic-update-slice_fusion.2
  388.2 2.0 convolution_bitcast_fusion.5
  390.2 2.0 convolution_bitcast_fusion.4
  392.2 1.5 copy_dynamic-update-slice_fusion.2
  398.4 2.0 convolution_bitcast_fusion.5
  400.4 2.0 convolution_bitcast_fusion.4
  402.4 1.5 copy_dynamic-update-slice_fusion.2
  408.5 2.0 convolution_bitcast_fusion.5
  410.5 2.0 convolution_bitcast_fusion.4
  412.6 1.5 copy_dynamic-update-slice_fusion.2
  418.7 2.0 convolution_bitcast_fusion.5
  420.7 2.0 convolution_bitcast_fusion.4
  (36 shorter events, 21.0 us)
Async XLA Ops:
  6.5 256.9 %all-gather.3.cloned.1.call-start = ((), (), s32[]{:S(2)}) async-start(), calls=%async_computation.1 | async-start | bytes 6291456 | tf_op jit(solution)/shard_map/all_gather | solution.py:103
  6.7 35.2 %copy-start = (s32[4,68608]{1,0:T(4,128)S(1)}, s32[4,68608]{1,0:T(4,128)}, u32[]{:S(2)}) copy-start(s32[4,68608]{1,0:T(4,128)} %param.6) | copy-start | bytes 3293188
  154.7 218.7 %all-gather.5.cloned.1.call-start = ((), (), s32[]{:S(2)}) async-start(), calls=%async_computation.2 | async-start | bytes 6291456 | tf_op jit(solution)/shard_map/all_gather | solution.py:104
  195.5 177.9 %copy-start.1 = (s32[10]{0:T(128)S(1)}, s32[10]{0:T(128)}, u32[]{:S(2)}) copy-start(s32[10]{0:T(128)} %constant.119.clone..sunk.2) | copy-start | bytes 124
  195.5 177.9 %copy-start.2 = (s32[10]{0:T(128)S(1)}, s32[10]{0:T(128)}, u32[]{:S(2)}) copy-start(s32[10]{0:T(128)} %constant.120.clone..sunk.2) | copy-start | bytes 124
  195.5 177.9 %copy-start.3 = (s32[10]{0:T(128)S(1)}, s32[10]{0:T(128)}, u32[]{:S(2)}) copy-start(s32[10]{0:T(128)} %param.7) | copy-start | bytes 124
Sparse Core Ops, SparseCore 0:
  154.8 108.6 all-gather.2
  265.3 108.0 all-gather.4
where the time goes:
time: 432 us; the launch traced here: 431 us
  waiting for transfers between devices  173 us (40%)
  other arithmetic  90.8 us (21%)
  blocking collectives  65.7 us (15%)
  local copies, waits for them, and re-layouts  46.9 us (11%)
  matrix products  34.6 us (8%)
  between operations  13.5 us (3%)
  loops' own time  6.67 us (2%)
    all_gather x1, waiting for transfers between devices, on_device(): lax.all_gather(twisted, 'grp', axis=3, tiled=True)  105 us
    all_gather x1, waiting for transfers between devices, on_device(): lax.all_gather(data, 'grp', axis=3, tiled=True)  68 us
    all_to_all x1, blocking collectives, on_device(): lax.all_to_all(channel_spectra, 'dev', split_axis=0, concat_axis=2, tiled...  65.7 us
    another operation x1, other arithmetic  35.2 us
    dot_general x1, matrix products, on_device(): jnp.einsum('aifn,nrc->ciarf', filtered, table, preferred_element_type=jnp...  14.4 us
    reduce_sum x10, other arithmetic, pick(): return jnp.sum(jnp.where(hits, table, 0)).astype(jnp.int32)  13.5 us
    another operation x1, other arithmetic, twist_parts(): jnp.stack([split[..., 1, :], -split[..., 0, :]], axis=-2)  12 us
    another operation x1, local copies, waits for them, and re-layouts, twist_parts(): jnp.stack([split[..., 1, :], -split[..., 0, :]], axis=-2)  10.6 us
  transfers between devices with their start and end apart: 2, of which 2 were waited for; matrix products, arithmetic and copies ran while one was open for 11% of the time, Pallas kernels for 0%

commit v1 on v0

v1 whole, which is shorter than its diff:
```python
import jax
import jax.numpy as jnp
import ml_dtypes
import numpy as np
from jax import lax
from jax.experimental import pallas as pl
from jax.experimental.pallas import tpu as pltpu
from jax.sharding import PartitionSpec as P

MESH = pl.DeviceIdType.MESH
BF16 = jnp.bfloat16
F32 = jnp.float32

A = 512
C = 1024
N = 2 * C
TAPS = 4
F = 64
I = 2
G = 2
LANES = 128
NB = N // LANES
LOCAL = 4
CH = 8
X = Z = Y = 4
K = 2
PLANE = X * Y * K
PIECE = CH * LOCAL
WORDS = 34304
TILES = WORDS // LANES
SLOTS = 5


def prototype():
    position = np.arange(TAPS * N) + 0.5
    window = 0.5 - 0.5 * np.cos(2.0 * np.pi * position / (N * TAPS))
    coeffs = (np.sinc(position / N - TAPS / 2.0) * window).astype(np.float32) / 64
    return coeffs.reshape(TAPS, NB, LANES).transpose(1, 0, 2).reshape(NB * TAPS, LANES)


def dft_table():
    index = (np.arange(C)[:, None] * np.arange(N)[None, :]) % N
    angle = 2.0 * np.pi / N * np.arange(N)
    factor = N**-0.5
    parts = np.stack([np.cos(angle) * factor, -np.sin(angle) * factor])
    parts = parts.astype(np.float32).astype(ml_dtypes.bfloat16)[:, index]
    parts = parts.reshape(2, X, Z, C // (X * Z), N).transpose(2, 0, 1, 3, 4)
    return np.ascontiguousarray(parts.reshape(Z, 2 * C // Z, N))


def front_kernel(v_hbm, coef, tab_hbm, s_hbm, v, x, fs, fb, tab, sf, s, sems):
    load = pltpu.make_async_copy(v_hbm, v, sems.at[0])
    load.start()
    tables = [pltpu.make_async_copy(tab_hbm.at[t], tab.at[t], sems.at[1 + t]) for t in range(Z)]
    load.wait()
    for table in tables:
        table.start()

    def unpack(tile, carry):
        at = pl.multiple_of(tile * LANES, LANES)
        words = jnp.concatenate([v[:, pl.ds(at, LANES)], v[:, pl.ds(at + WORDS, LANES)]], axis=0)
        for byte in range(4):
            raw = jnp.bitwise_and(jnp.right_shift(words, 8 * byte), 255) - 128
            x[byte * TILES + tile] = raw.astype(F32)
        return carry

    lax.fori_loop(0, TILES, unpack, 0, unroll=4)

    def fir(nb, carry):
        c = [coef[pl.ds(nb * TAPS + k, 1), :] for k in range(TAPS)]
        window = [x[k * NB + nb] for k in range(TAPS - 1)]
        for f in range(F):
            window.append(x[(f + TAPS - 1) * NB + nb])
            total = window[0] * c[0]
            for k in range(1, TAPS):
                total = total + window[k] * c[k]
            window.pop(0)
            fs[pl.ds(f, 8, stride=F), :] = total
        fb[:, pl.ds(pl.multiple_of(nb * LANES, LANES), LANES)] = fs[...].astype(BF16)
        return carry

    lax.fori_loop(0, NB, fir, 0)

    low = lax.broadcasted_iota(jnp.int32, (C // Z, LANES), 1) < F
    rows = C // Z
    outs = []
    for t in range(Z):
        tables[t].wait()
        spectra = lax.dot_general(
            tab[t], fb[...], (((1,), (1,)), ((), ())), preferred_element_type=F32
        )
        for i in range(I):
            for pair in range(LOCAL // 2):
                tile = (i * LOCAL // 2 + pair) * LANES
                re = spectra[:rows, tile : tile + LANES]
                im = spectra[rows:, tile : tile + LANES]
                even = jnp.where(low, re, pltpu.roll(im, F, 1))
                odd = jnp.where(low, pltpu.roll(re, F, 1), im)
                sf[i, pl.ds(2 * pair, rows, stride=LOCAL), :] = even
                sf[i, pl.ds(2 * pair + 1, rows, stride=LOCAL), :] = odd
            s[t, :, i] = sf[i].reshape(PLANE, PIECE, LANES).astype(BF16)
        out = pltpu.make_async_copy(s.at[t], s_hbm.at[t], sems.at[1 + Z + t])
        out.start()
        outs.append(out)
    for out in outs:
        out.wait()


def front(voltages):
    coef = jnp.asarray(prototype())
    table = jnp.asarray(dft_table())
    return pl.pallas_call(
        front_kernel,
        name="front",
        out_shape=jax.ShapeDtypeStruct((Z, PLANE, I, PIECE, LANES), BF16),
        in_specs=[
            pl.BlockSpec(memory_space=pl.ANY),
            pl.BlockSpec(memory_space=pltpu.VMEM),
            pl.BlockSpec(memory_space=pl.ANY),
        ],
        out_specs=pl.BlockSpec(memory_space=pl.ANY),
        scratch_shapes=[
            pltpu.VMEM((LOCAL, I * WORDS), jnp.int32),
            pltpu.VMEM((4 * TILES, I * LOCAL, LANES), F32),
            pltpu.VMEM((I * LOCAL * F, LANES), F32),
            pltpu.VMEM((I * LOCAL * F, N), BF16),
            pltpu.VMEM((Z, 2 * C // Z, N), BF16),
            pltpu.VMEM((I, C // Z * LOCAL, LANES), F32),
            pltpu.VMEM((Z, PLANE, I, PIECE, LANES), BF16),
            pltpu.SemaphoreType.DMA((1 + 2 * Z,)),
        ],
        compiler_params=pltpu.CompilerParams(vmem_limit_bytes=48 * 1024 * 1024),
    )(voltages, coef, table)


ORDER = (0, 2, 1, 3)


def turn_kernel(s, r, b, c, hop, plane_send, plane_recv, own_sem, send, recv, hop_send, hop_recv, far_send, far_recv):
    grp = lax.axis_index("grp")
    dev = lax.axis_index("dev")
    x, z, y, k = dev // 32, (dev // 8) % 4, (dev // 2) % 4, dev % 2

    def at_plane(n):
        place = (x * 8 + y * 2 + k) ^ n
        return place, (grp, (place // 8) * 32 + z * 8 + place % 8)

    def at_ring(height):
        height = lax.rem(height + 2 * Z, 2 * Z)
        return (height // Z, x * 32 + (height % Z) * 8 + y * 2 + k)

    here = grp * Z + z
    mine = x * 8 + y * 2 + k

    barrier = pltpu.get_barrier_semaphore()

    def greet_plane(n, carry):
        _, device = at_plane(n)
        pl.semaphore_signal(barrier, inc=1, device_id=device, device_id_type=MESH)
        return carry

    def greet_ring(n, carry):
        pl.semaphore_signal(barrier, inc=1, device_id=at_ring(here + n), device_id_type=MESH)
        return carry

    lax.fori_loop(1, PLANE, greet_plane, 0)
    lax.fori_loop(1, G * Z, greet_ring, 0)
    pl.semaphore_wait(barrier, PLANE + G * Z - 2)

    def target(step):
        return lax.rem(z + step, Z)

    own = []
    for j, step in enumerate(ORDER):
        t = target(step)

        def spread(n, carry):
            place, device = at_plane(n)
            pltpu.make_async_remote_copy(
                s.at[t, place], b.at[j, mine], plane_send.at[j], plane_recv.at[j], device, MESH
            ).start()
            return carry

        lax.fori_loop(1, PLANE, spread, 0)
        copy = pltpu.make_async_copy(s.at[t, mine], b.at[j, mine], own_sem.at[j])
        copy.start()
        own.append(copy)

    row = lax.broadcasted_iota(jnp.int32, (256, 256), 0)
    col = lax.broadcasted_iota(jnp.int32, (256, 256), 1)
    source = ((row >> 2) & 7) * 32 + (row >> 5) * 4 + (row & 3)
    order = (source == col).astype(F32).astype(BF16)

    sends = []
    half = CH * X
    for j, step in enumerate(ORDER):
        own[j].wait()
        whole = pl.ds(0, PLANE - 1)
        pltpu.make_async_copy(b.at[j, whole], b.at[j, whole], plane_recv.at[j]).wait()
        for xs in range(X):
            pieces = [b[j, xs * 8 : xs * 8 + 8, i].reshape(256, LANES) for i in range(I)]
            mixed = jnp.dot(order, jnp.concatenate(pieces, axis=1), preferred_element_type=F32)
            for i in range(I):
                part = mixed[:, i * LANES : (i + 1) * LANES].astype(BF16)
                c[j, i, :, xs] = part.reshape(CH, PIECE, LANES)
        if step == 0:
            copy = pltpu.make_async_copy(c.at[j], r.at[grp, :, :, :, z], own_sem.at[j])
            copy.start()
            local = copy
            for i, way in enumerate((1, -1)):
                copy = pltpu.make_async_remote_copy(
                    c.at[j, i], hop.at[i], hop_send.at[i], hop_recv.at[i], at_ring(here + way), MESH
                )
                copy.start()
                sends.append(copy)
        else:
            for other in range(G):
                to = lax.rem(grp + other, G)
                copy = pltpu.make_async_remote_copy(
                    c.at[j],
                    r.at[grp, :, :, :, z],
                    send.at[j, other],
                    recv.at[j, other],
                    at_ring(to * Z + target(step)),
                    MESH,
                )
                copy.start()
                sends.append(copy)
        if j == 1:
            for i, way in enumerate((1, -1)):
                sends[i].wait_recv()
                origin = lax.rem(here - way + G * Z, G * Z)
                copy = pltpu.make_async_remote_copy(
                    hop.at[i],
                    r.at[origin // Z, i, :, :, origin % Z],
                    far_send.at[i],
                    far_recv.at[i],
                    at_ring(here + 3 * way),
                    MESH,
                )
                copy.start()
                sends.append(copy)
    local.wait()
    for copy in sends[:2]:
        copy.wait_send()
    for copy in sends[2:]:
        copy.wait()
    for j in range(Z):
        whole = pl.ds(0, PLANE - 1)
        pltpu.make_async_copy(s.at[0, whole], s.at[0, whole], plane_send.at[j]).wait()


def turn(spectra):
    return pl.pallas_call(
        turn_kernel,
        name="turn",
        out_shape=jax.ShapeDtypeStruct((G, I, CH, X, Z, PIECE, LANES), BF16),
        in_specs=[pl.BlockSpec(memory_space=pl.ANY)],
        out_specs=pl.BlockSpec(memory_space=pl.ANY),
        scratch_shapes=[
            pltpu.VMEM((Z, PLANE, I, PIECE, LANES), BF16),
            pltpu.VMEM((Z, I, CH, X, PIECE, LANES), BF16),
            pltpu.VMEM((I, CH, X, PIECE, LANES), BF16),
            pltpu.SemaphoreType.DMA((Z,)),
            pltpu.SemaphoreType.DMA((Z,)),
            pltpu.SemaphoreType.DMA((Z,)),
            pltpu.SemaphoreType.DMA((Z, G)),
            pltpu.SemaphoreType.DMA((Z, G)),
            pltpu.SemaphoreType.DMA((2,)),
            pltpu.SemaphoreType.DMA((2,)),
            pltpu.SemaphoreType.DMA((2,)),
            pltpu.SemaphoreType.DMA((2,)),
        ],
        compiler_params=pltpu.CompilerParams(
            collective_id=0, has_side_effects=True, vmem_limit_bytes=48 * 1024 * 1024
        ),
    )(spectra)


def gram_kernel(order, r_hbm, out, r, sems):
    i, s = pl.program_id(0), pl.program_id(1)
    loads = [pltpu.make_async_copy(r_hbm.at[:, n], r.at[n], sems.at[n]) for n in range(I)]

    @pl.when((i == 0) & (s == 0))
    def _():
        for load in loads:
            load.start()

    for n in range(I):

        @pl.when((i == n) & (s == 0))
        def _(n=n):
            loads[n].wait()

    entry = order[lax.axis_index("grp") * SLOTS + s]
    one = lambda bound: (entry >= bound).astype(jnp.int32)
    p = one(4) + one(7) + one(9)
    q = entry - (3 * one(4) + 2 * one(7) + one(9))

    for ch in range(CH):
        left, twisted, right = [], [], []
        for g in range(G):
            block = r[i, g, ch, p]
            wide = block.astype(F32)
            left.append(block)
            twisted.append(jnp.concatenate([wide[:, F:], -wide[:, :F]], axis=1).astype(BF16))
            right.append(r[i, g, ch, q])
        both = jnp.concatenate(
            [jnp.concatenate(left, axis=1), jnp.concatenate(twisted, axis=1)], axis=0
        )
        sums = lax.dot_general(
            both,
            jnp.concatenate(right, axis=1),
            (((1,), (1,)), ((), ())),
            preferred_element_type=F32,
        )
        sums = sums * (1.0 / (G * F))
        out[0, 0, 0, ch] = sums[:LANES]
        out[0, 0, 1, ch] = sums[LANES:]


def gram(block_order, data):
    return pl.pallas_call(
        gram_kernel,
        name="gram",
        out_shape=jax.ShapeDtypeStruct((SLOTS, I, 2, CH, LANES, LANES), F32),
        grid_spec=pltpu.PrefetchScalarGridSpec(
            num_scalar_prefetch=1,
            grid=(I, SLOTS),
            in_specs=[pl.BlockSpec(memory_space=pl.ANY)],
            out_specs=pl.BlockSpec(
                (1, 1, 2, CH, LANES, LANES), lambda i, s, order: (s, i, 0, 0, 0, 0)
            ),
            scratch_shapes=[
                pltpu.VMEM((I, G, CH, X, LANES, LANES), BF16),
                pltpu.SemaphoreType.DMA((I,)),
            ],
        ),
        compiler_params=pltpu.CompilerParams(vmem_limit_bytes=48 * 1024 * 1024),
    )(block_order, data)


def on_device(voltages, block_order):
    spectra = front(voltages)
    data = turn(spectra)
    return gram(block_order, data.reshape(G, I, CH, X, LANES, LANES))


def solution(mesh):
    in_specs = (P("dev", "grp"), P())
    out_specs = P("grp", None, None, "dev", None, None)
    return jax.shard_map(
        on_device, mesh=mesh, in_specs=in_specs, out_specs=out_specs, check_vma=False
    )
```

time: 432 us -> 138 us (0.32)
  waiting for transfers between devices: 173 us -> 0 us
  Pallas kernels: 0 us -> 134 us
  other arithmetic: 90.8 us -> 0 us
  blocking collectives: 65.7 us -> 0 us
  local copies, waits for them, and re-layouts: 46.9 us -> 4.19 us
  matrix products: 34.6 us -> 0 us
  between operations: 13.5 us -> 0.04 us
  loops' own time: 6.67 us -> 0 us
    all_gather x2 -> x0, waiting for transfers between devices: 173 us -> none  [the longest x1 105 us: on_device(): lax.all_gather(twisted, 'grp', axis=3, tiled=True)]
    pallas_call x0 -> x3, Pallas kernels: none -> 134 us  [the longest x1 114 us: turn(): pl.pallas_call(turn_kernel, name='turn', out_shape=jax.ShapeDtypeStruct((...]
    all_to_all x1 -> x0, blocking collectives: 65.7 us -> none  [on_device(): lax.all_to_all(channel_spectra, 'dev', split_axis=0, concat_axis=2, tiled...]
    another operation x2 -> x0, other arithmetic: 47.2 us -> none
    dot_general x11 -> x0, matrix products: 34.6 us -> none  [the longest x1 14.4 us: on_device(): jnp.einsum('aifn,nrc->ciarf', filtered, table, preferred_element_type=jnp...]
    reshape x3 -> x0, local copies, waits for them, and re-layouts: 18 us -> none  [the longest x1 8.43 us: twist_parts(): data.reshape(data.shape[:3] + (width // (2 * BLOCK_FRAMES), 2, BLOCK_FRAM...]
    reduce_sum x10 -> x0, other arithmetic: 13.5 us -> none  [pick(): return jnp.sum(jnp.where(hits, table, 0)).astype(jnp.int32)]
    another operation x1 -> x0, local copies, waits for them, and re-layouts: 10.6 us -> none  [twist_parts(): jnp.stack([split[..., 1, :], -split[..., 0, :]], axis=-2)]
  transfers between devices with their start and end apart: 2 -> 0, of which waited for: 2 -> 0; matrix products, arithmetic and copies ran while one was open for 11% -> 0% of each run, Pallas kernels for 0% -> 0%
where the time goes in v1:
time: 138 us
  Pallas kernels  134 us (97%)
  local copies, waits for them, and re-layouts  4.19 us (3%)
    pallas_call x1, Pallas kernels, turn(): pl.pallas_call(turn_kernel, name='turn', out_shape=jax.ShapeDtypeStruct((...  114 us
    pallas_call x1, Pallas kernels, front(): pl.pallas_call(front_kernel, name='front', out_shape=jax.ShapeDtypeStruct...  11 us
    pallas_call x1, Pallas kernels, gram(): pl.pallas_call(gram_kernel, name='gram', out_shape=jax.ShapeDtypeStruct((...  8.93 us
    unnamed x8, local copies, waits for them, and re-layouts  4.19 us

profile of v1, /device:TPU:1, one launch (start us, length us, event | category | flops | bytes accessed | tf_op | source)
XLA Modules:
  0.0 138.2 jit_solution(1643436048836367327)
XLA Ops:
  0.0 0.0 copy-start.1
  0.0 1.2 copy-done.1
  1.2 0.0 copy-start.2
  1.2 0.8 copy-done.2
  2.0 11.0 %front.1.s = bf16[4,32,2,32,128]{4,3,2,1,0:T(8,128)(2,1)S(1)} custom-call(s32[4,68608]{1,0:T(4,128)S(1)} %copy-done.1, f32[64,128]{1,0:T(8,128)S(1)} %copy-done.2, bf16[4,512,2048]{2,1,0:T(8,128)(2,1)} %constant.5.clone.tab_hbm), custom_call_target="tpu_custom_call" | custom-call | tf_op jit(solution)/shard_map/front/pallas_call | solution.py:112
  13.0 0.0 copy-start.3
  13.0 114.1 %turn.1 = bf16[2,2,8,4,4,32,128]{6,5,4,3,2,1,0:T(8,128)(2,1)} custom-call(bf16[4,32,2,32,128]{4,3,2,1,0:T(8,128)(2,1)S(1)} %front.1.s), custom_call_target="tpu_custom_call" | custom-call | tf_op jit(solution)/shard_map/turn/pallas_call | solution.py:254
  127.1 0.0 copy-done.3
  127.1 0.0 copy-start
  127.1 2.2 %copy-done = bf16[2,2,8,4,4,32,128]{6,5,4,3,2,1,0:T(8,128)(2,1)S(1)} copy-done((bf16[2,2,8,4,4,32,128]{6,5,4,3,2,1,0:T(8,128)(2,1)S(1)}, bf16[2,2,8,4,4,32,128]{6,5,4,3,2,1,0:T(8,128)(2,1)}, u32[]{:S(2)}) %copy-start) | copy-done | bytes 4194328
  129.3 8.9 %gram.1 = f32[5,2,2,8,128,128]{5,4,3,2,1,0:T(8,128)} custom-call(s32[10]{0:T(128)S(1)} %copy-done.3, bf16[2,2,8,4,128,128]{5,4,3,2,1,0:T(8,128)(2,1)S(1)} %bitcast.1), custom_call_target="tpu_custom_call" | custom-call | tf_op jit(solution)/shard_map/gram/pallas_call | solution.py:323
Async XLA Ops:
  0.0 1.2 copy-start.1
  1.2 0.8 copy-start.2
  13.0 114.1 %copy-start.3 = (s32[10]{0:T(128)S(1)}, s32[10]{0:T(128)}, u32[]{:S(2)}) copy-start(s32[10]{0:T(128)} %order.1) | copy-start | bytes 124
  127.1 2.2 %copy-start = (bf16[2,2,8,4,4,32,128]{6,5,4,3,2,1,0:T(8,128)(2,1)S(1)}, bf16[2,2,8,4,4,32,128]{6,5,4,3,2,1,0:T(8,128)(2,1)}, u32[]{:S(2)}) copy-start(bf16[2,2,8,4,4,32,128]{6,5,4,3,2,1,0:T(8,128)(2,1)} %turn.1) | copy-start | bytes 12582916

commit v2 on v0

v2 whole, which is shorter than its diff:
```python
import jax
import jax.numpy as jnp
import ml_dtypes
import numpy as np
from jax import lax
from jax.experimental import pallas as pl
from jax.experimental.pallas import tpu as pltpu
from jax.sharding import PartitionSpec as P

MESH = pl.DeviceIdType.MESH
BF16 = jnp.bfloat16
F32 = jnp.float32

A = 512
C = 1024
N = 2 * C
TAPS = 4
F = 64
I = 2
G = 2
LANES = 128
NB = N // LANES
LOCAL = 4
CH = 8
X = Z = Y = 4
PLANE = X * Y * 2
H = 2
HC = CH // H
PIECE = HC * LOCAL
ROWS = 8 * LOCAL
UNITS = H * Z
STEP = F + 8
SPLIT = 2
WORDS = 34304
TILES = WORDS // LANES
SLOTS = 5


def prototype():
    position = np.arange(TAPS * N) + 0.5
    window = 0.5 - 0.5 * np.cos(2.0 * np.pi * position / (N * TAPS))
    coeffs = (np.sinc(position / N - TAPS / 2.0) * window).astype(np.float32) / 64
    return coeffs.reshape(TAPS, NB, LANES).transpose(1, 0, 2).reshape(NB * TAPS, LANES)


def dft_table():
    index = (np.arange(C)[:, None] * np.arange(N)[None, :]) % N
    angle = 2.0 * np.pi / N * np.arange(N)
    factor = N**-0.5
    parts = np.stack([np.cos(angle) * factor, -np.sin(angle) * factor])
    parts = parts.astype(np.float32).astype(ml_dtypes.bfloat16)[:, index]
    parts = parts.reshape(2, X, Z, 8, H, HC, N).transpose(2, 4, 0, 1, 3, 5, 6)
    return np.ascontiguousarray(parts.reshape(Z, H, 2 * C // UNITS, N))


def correlate(order, slot, block, store):
    entry = order[slot]
    one = lambda bound: (entry >= bound).astype(jnp.int32)
    p = one(4) + one(7) + one(9)
    q = entry - (3 * one(4) + 2 * one(7) + one(9))
    for i in range(I):
        for ch in range(HC):
            left, twisted, right = [], [], []
            for g in range(G):
                data = block(g, i, ch, p)
                wide = data.astype(F32)
                left.append(data)
                twisted.append(jnp.concatenate([wide[:, F:], -wide[:, :F]], axis=1).astype(BF16))
                right.append(block(g, i, ch, q))
            both = jnp.concatenate(
                [jnp.concatenate(left, axis=1), jnp.concatenate(twisted, axis=1)], axis=0
            )
            sums = lax.dot_general(
                both,
                jnp.concatenate(right, axis=1),
                (((1,), (1,)), ((), ())),
                preferred_element_type=F32,
            )
            sums = sums * (1.0 / (G * F))
            store(i, ch, sums[:LANES], sums[LANES:])


def step_of(u):
    return 2 * ((u % Z) % 2) + (u % Z) // 2


def main_kernel(
    order, v_hbm, coef_hbm, tab_hbm, early, late, v, coef, x, fs, fb, tab, sf, s, b, c, r,
    load_sem, tab_sem, plane_send, plane_recv, send, recv,
):
    grp = lax.axis_index("grp")
    dev = lax.axis_index("dev")
    z = (dev // 8) % 4
    mine = (dev // 32) * 8 + dev % 8
    here = grp * Z + z

    def at_plane(n):
        place = mine ^ n
        return place, (grp, (place // 8) * 32 + z * 8 + place % 8)

    def at_ring(height):
        height = lax.rem(height, G * Z)
        return (height // Z, (dev // 32) * 32 + (height % Z) * 8 + dev % 8)

    width = WORDS // SPLIT
    loads = [pltpu.make_async_copy(coef_hbm, coef, load_sem.at[0])]
    for part in range(SPLIT):
        for i in range(I):
            span = pl.ds(i * WORDS + part * width, width)
            n = 1 + part * I + i
            loads.append(pltpu.make_async_copy(v_hbm.at[:, span], v.at[:, span], load_sem.at[n]))
    for load in loads:
        load.start()

    barrier = pltpu.get_barrier_semaphore()

    def greet_plane(n, carry):
        _, device = at_plane(n)
        pl.semaphore_signal(barrier, inc=1, device_id=device, device_id_type=MESH)
        return carry

    def greet_ring(n, carry):
        pl.semaphore_signal(barrier, inc=1, device_id=at_ring(here + n), device_id_type=MESH)
        return carry

    lax.fori_loop(1, PLANE, greet_plane, 0)
    lax.fori_loop(1, G * Z, greet_ring, 0)

    def unpack(tile, carry):
        at = pl.multiple_of(tile * LANES, LANES)
        words = jnp.concatenate([v[:, pl.ds(at, LANES)], v[:, pl.ds(at + WORDS, LANES)]], axis=0)
        for byte in range(4):
            raw = jnp.bitwise_and(jnp.right_shift(words, 8 * byte), 255) - 128
            x[byte * TILES + tile] = raw.astype(F32)
        return carry

    def table_copy(u):
        t = (z + step_of(u)) % Z
        return pltpu.make_async_copy(tab_hbm.at[t, u // Z], tab.at[u], tab_sem.at[u])

    for part in range(SPLIT):
        for i in range(I):
            loads[1 + part * I + i].wait()
        if part == SPLIT - 1:
            for u in range(UNITS):
                table_copy(u).start()
        tiles = TILES // SPLIT
        lax.fori_loop(part * tiles, (part + 1) * tiles, unpack, 0, unroll=2)
    loads[0].wait()

    def fir(nb, carry):
        taps = [coef[pl.ds(nb * TAPS + k, 1), :] for k in range(TAPS)]
        window = [x[k * NB + nb] for k in range(TAPS - 1)]
        for f in range(F):
            window.append(x[(f + TAPS - 1) * NB + nb])
            total = window[0] * taps[0]
            for k in range(1, TAPS):
                total = total + window[k] * taps[k]
            window.pop(0)
            fs[pl.ds(f, 8, stride=STEP), :] = total
        at = pl.ds(pl.multiple_of(nb * LANES, LANES), LANES)
        for row in range(I * LOCAL):
            fb[row * F : (row + 1) * F, at] = fs[row * STEP : row * STEP + F, :].astype(BF16)
        return carry

    lax.fori_loop(0, NB, fir, 0)
    pl.semaphore_wait(barrier, PLANE + G * Z - 2)

    rows = C // UNITS
    low = lax.broadcasted_iota(jnp.int32, (rows, LANES), 1) < F

    def make(u, carry):
        table_copy(u).wait()
        spectra = lax.dot_general(
            tab[u], fb[...], (((1,), (1,)), ((), ())), preferred_element_type=F32
        )
        for i in range(I):
            for pair in range(LOCAL // 2):
                tile = (i * LOCAL // 2 + pair) * LANES
                re = spectra[:rows, tile : tile + LANES]
                im = spectra[rows:, tile : tile + LANES]
                even = jnp.where(low, re, pltpu.roll(im, F, 1))
                odd = jnp.where(low, pltpu.roll(re, F, 1), im)
                sf[i, pl.ds(2 * pair, rows, stride=LOCAL), :] = even
                sf[i, pl.ds(2 * pair + 1, rows, stride=LOCAL), :] = odd
            s[u, :, i] = sf[i].reshape(PLANE, PIECE, LANES).astype(BF16)

        def spread(n, carry):
            place, device = at_plane(n)
            pltpu.make_async_remote_copy(
                s.at[u, place], b.at[u, mine], plane_send.at[u], plane_recv.at[u], device, MESH
            ).start()
            return carry

        lax.fori_loop(1, PLANE, spread, 0)
        b[u, mine] = s[u, mine]
        return carry

    row = lax.broadcasted_iota(jnp.int32, (256, 256), 0)
    col = lax.broadcasted_iota(jnp.int32, (256, 256), 1)
    source = (row // 128) * 128 + ((row // 4) % 8) * 16 + ((row // 32) % 4) * 4 + row % 4
    swap = (source == col).astype(F32).astype(BF16)

    halves = (r, late)

    def ring_copy(half, u, other):
        to = lax.rem(grp + other, G)
        step = step_of(u)
        return pltpu.make_async_remote_copy(
            c.at[u],
            halves[half].at[grp, :, :, :, z],
            send.at[u, other],
            recv.at[u, other],
            at_ring(to * Z + (z + step) % Z),
            MESH,
        )

    def pass_on(half, u):
        whole = pl.ds(0, PLANE - 1)
        pltpu.make_async_copy(b.at[u, whole], b.at[u, whole], plane_recv.at[u]).wait()
        for pair in range(X // 2):
            pieces = [
                b[u, pair * 16 : pair * 16 + 16, i].reshape(256, LANES) for i in range(I)
            ]
            mixed = jnp.dot(swap, jnp.concatenate(pieces, axis=1), preferred_element_type=F32)
            for i in range(I):
                part = mixed[:, i * LANES : (i + 1) * LANES].astype(BF16)
                part = part.reshape(2, HC, ROWS, LANES)
                for n in range(2):
                    c[u, i, :, pair * 2 + n] = part[n]
        ring_copy(half, u, 1).start()

        @pl.when(u % Z == 0)
        def _():
            halves[half][grp, :, :, :, z] = c[u]

        @pl.when(u % Z != 0)
        def _():
            ring_copy(half, u, 0).start()

    lax.fori_loop(0, Z, make, 0)

    def both(u, carry):
        pass_on(0, u)
        return make(u + Z, carry)

    lax.fori_loop(0, Z, both, 0)

    def rest(u, carry):
        pass_on(1, u)
        return carry

    lax.fori_loop(Z, UNITS, rest, 0)

    def arrive(half):
        def one(u, carry):
            ring_copy(half, u, 1).wait_recv()

            @pl.when(u % Z != 0)
            def _():
                ring_copy(half, u, 0).wait_recv()

            return carry

        lax.fori_loop(half * Z, half * Z + Z, one, 0)

    arrive(0)

    def early_slot(n, carry):
        def block(g, i, ch, p):
            return r[g, i, ch, p].reshape(LANES, LANES)

        def store(i, ch, re, im):
            early[n, i, 0, ch] = re
            early[n, i, 1, ch] = im

        correlate(order, grp * SLOTS + n, block, store)
        return carry

    lax.fori_loop(0, SLOTS, early_slot, 0)
    arrive(1)

    def sent(u, carry):
        ring_copy(0, u, 1).wait_send()

        @pl.when(u % Z != 0)
        def _():
            ring_copy(0, u, 0).wait_send()

        whole = pl.ds(0, PLANE - 1)
        pltpu.make_async_copy(s.at[u, whole], s.at[u, whole], plane_send.at[u]).wait()
        return carry

    lax.fori_loop(0, UNITS, sent, 0)


def main(block_order, voltages):
    coef = jnp.asarray(prototype())
    table = jnp.asarray(dft_table())
    hbm = pl.BlockSpec(memory_space=pltpu.HBM)
    return pl.pallas_call(
        main_kernel,
        name="main",
        out_shape=(
            pltpu.VMEM((SLOTS, I, 2, HC, LANES, LANES), F32),
            pltpu.VMEM((G, I, HC, X, Z, ROWS, LANES), BF16),
        ),
        in_specs=[pl.BlockSpec(memory_space=pltpu.SMEM), hbm, hbm, hbm],
        out_specs=(pl.BlockSpec(memory_space=pltpu.VMEM), pl.BlockSpec(memory_space=pltpu.VMEM)),
        scratch_shapes=[
            pltpu.VMEM((LOCAL, I * WORDS), jnp.int32),
            pltpu.VMEM((NB * TAPS, LANES), F32),
            pltpu.VMEM((4 * TILES, I * LOCAL, LANES), F32),
            pltpu.VMEM((I * LOCAL * STEP, LANES), F32),
            pltpu.VMEM((I * LOCAL * F, N), BF16),
            pltpu.VMEM((UNITS, 2 * C // UNITS, N), BF16),
            pltpu.VMEM((I, C // UNITS * LOCAL, LANES), F32),
            pltpu.VMEM((UNITS, PLANE, I, PIECE, LANES), BF16),
            pltpu.VMEM((UNITS, PLANE, I, PIECE, LANES), BF16),
            pltpu.VMEM((UNITS, I, HC, X, ROWS, LANES), BF16),
            pltpu.VMEM((G, I, HC, X, Z, ROWS, LANES), BF16),
            pltpu.SemaphoreType.DMA((1 + SPLIT * I,)),
            pltpu.SemaphoreType.DMA((UNITS,)),
            pltpu.SemaphoreType.DMA((UNITS,)),
            pltpu.SemaphoreType.DMA((UNITS,)),
            pltpu.SemaphoreType.DMA((UNITS, G)),
            pltpu.SemaphoreType.DMA((UNITS, G)),
        ],
        compiler_params=pltpu.CompilerParams(
            collective_id=0, has_side_effects=True, vmem_limit_bytes=48 * 1024 * 1024
        ),
    )(block_order, voltages, coef, table)


def last_kernel(order, early, late, out, results, early_sem, sems):
    first = pltpu.make_async_copy(early, out.at[:, :, :, pl.ds(0, HC)], early_sem)
    first.start()
    grp = lax.axis_index("grp")

    def result(n):
        return pltpu.make_async_copy(results.at[n], out.at[n, :, :, pl.ds(HC, HC)], sems.at[n])

    def slot(n, carry):
        def block(g, i, ch, p):
            return late[g, i, ch, p].reshape(LANES, LANES)

        def store(i, ch, re, im):
            results[n, i, 0, ch] = re
            results[n, i, 1, ch] = im

        correlate(order, grp * SLOTS + n, block, store)
        result(n).start()
        return carry

    lax.fori_loop(0, SLOTS, slot, 0)
    first.wait()
    for n in range(SLOTS):
        result(n).wait()


def last(block_order, early, late):
    vmem = pl.BlockSpec(memory_space=pltpu.VMEM)
    return pl.pallas_call(
        last_kernel,
        name="last",
        out_shape=jax.ShapeDtypeStruct((SLOTS, I, 2, CH, LANES, LANES), F32),
        in_specs=[pl.BlockSpec(memory_space=pltpu.SMEM), vmem, vmem],
        out_specs=pl.BlockSpec(memory_space=pltpu.HBM),
        scratch_shapes=[
            pltpu.VMEM((SLOTS, I, 2, HC, LANES, LANES), F32),
            pltpu.SemaphoreType.DMA,
            pltpu.SemaphoreType.DMA((SLOTS,)),
        ],
        compiler_params=pltpu.CompilerParams(vmem_limit_bytes=24 * 1024 * 1024),
    )(block_order, early, late)


def on_device(voltages, block_order):
    early, late = main(block_order, voltages)
    return last(block_order, early, late)


def solution(mesh):
    in_specs = (P("dev", "grp"), P())
    out_specs = P("grp", None, None, "dev", None, None)
    return jax.shard_map(
        on_device, mesh=mesh, in_specs=in_specs, out_specs=out_specs, check_vma=False
    )
```

time: 432 us -> 120 us (0.28)
  waiting for transfers between devices: 173 us -> 0 us
  Pallas kernels: 0 us -> 120 us
  other arithmetic: 90.8 us -> 0 us
  blocking collectives: 65.7 us -> 0 us
  local copies, waits for them, and re-layouts: 46.9 us -> 0.01 us
  matrix products: 34.6 us -> 0 us
  between operations: 13.5 us -> 0.02 us
  loops' own time: 6.67 us -> 0 us
    all_gather x2 -> x0, waiting for transfers between devices: 173 us -> none  [the longest x1 105 us: on_device(): lax.all_gather(twisted, 'grp', axis=3, tiled=True)]
    pallas_call x0 -> x2, Pallas kernels: none -> 120 us  [the longest x1 116 us: main(): pl.pallas_call(main_kernel, name='main', out_shape=(pltpu.VMEM((SLOTS, I,...]
    all_to_all x1 -> x0, blocking collectives: 65.7 us -> none  [on_device(): lax.all_to_all(channel_spectra, 'dev', split_axis=0, concat_axis=2, tiled...]
    another operation x2 -> x0, other arithmetic: 47.2 us -> none
    dot_general x11 -> x0, matrix products: 34.6 us -> none  [the longest x1 14.4 us: on_device(): jnp.einsum('aifn,nrc->ciarf', filtered, table, preferred_element_type=jnp...]
    reshape x3 -> x0, local copies, waits for them, and re-layouts: 18 us -> none  [the longest x1 8.43 us: twist_parts(): data.reshape(data.shape[:3] + (width // (2 * BLOCK_FRAMES), 2, BLOCK_FRAM...]
    reduce_sum x10 -> x0, other arithmetic: 13.5 us -> none  [pick(): return jnp.sum(jnp.where(hits, table, 0)).astype(jnp.int32)]
    another operation x1 -> x0, local copies, waits for them, and re-layouts: 10.6 us -> none  [twist_parts(): jnp.stack([split[..., 1, :], -split[..., 0, :]], axis=-2)]
  transfers between devices with their start and end apart: 2 -> 0, of which waited for: 2 -> 0; matrix products, arithmetic and copies ran while one was open for 11% -> 0% of each run, Pallas kernels for 0% -> 0%
where the time goes in v2:
time: 120 us
  Pallas kernels  120 us (100%)
    pallas_call x1, Pallas kernels, main(): pl.pallas_call(main_kernel, name='main', out_shape=(pltpu.VMEM((SLOTS, I,...  116 us
    pallas_call x1, Pallas kernels, last(): pl.pallas_call(last_kernel, name='last', out_shape=jax.ShapeDtypeStruct((...  4.55 us

profile of v2, /device:TPU:1, one launch (start us, length us, event | category | flops | bytes accessed | tf_op | source)
XLA Modules:
  0.0 120.1 jit_solution(17796254762745430031)
XLA Ops:
  0.0 0.0 copy-start
  0.0 115.5 %main.1 = (f32[5,2,2,4,128,128]{5,4,3,2,1,0:T(8,128)S(1)}, bf16[2,2,4,4,4,32,128]{6,5,4,3,2,1,0:T(8,128)(2,1)S(1)}) custom-call(s32[10]{0:T(128)} %order.3, s32[4,68608]{1,0:T(4,128)} %v_hbm.1, f32[64,128]{1,0:T(8,128)} %constant.4.clone.coef_hbm, bf16[4,2,256,2048]{3,2,1,0:T(8,128)(2,1)} %constant.5.clone.tab_hbm), custom_call_target="tpu_custom_call" | custom-call | tf_op jit(solution)/shard_map/main/pallas_call | solution.py:301
  115.6 0.0 copy-done
  115.6 4.5 %last.1 = f32[5,2,2,8,128,128]{5,4,3,2,1,0:T(8,128)} custom-call(s32[10]{0:T(128)S(1)} %copy-done, f32[5,2,2,4,128,128]{5,4,3,2,1,0:T(8,128)S(1)} %get-tuple-element.7.early, bf16[2,2,4,4,4,32,128]{6,5,4,3,2,1,0:T(8,128)(2,1)S(1)} %get-tuple-element.8.late), custom_call_target="tpu_custom_call" | custom-call | tf_op jit(solution)/shard_map/last/pallas_call | solution.py:363
Async XLA Ops:
  0.0 115.6 %copy-start = (s32[10]{0:T(128)S(1)}, s32[10]{0:T(128)}, u32[]{:S(2)}) copy-start(s32[10]{0:T(128)} %order.3) | copy-start | bytes 124

commit v3 on v2

--- a/solution.py
+++ b/solution.py
@@ -24,11 +24,12 @@
 CH = 8
 X = Z = Y = 4
 PLANE = X * Y * 2
-H = 2
-HC = CH // H
-PIECE = HC * LOCAL
+Q = 4
+QC = CH // Q
+PIECE = QC * I * LOCAL
+EARLY = (Q - 1) * QC
 ROWS = 8 * LOCAL
-UNITS = H * Z
+UNITS = Q * Z
 STEP = F + 8
 SPLIT = 2
 WORDS = 34304
@@ -49,8 +50,8 @@
     factor = N**-0.5
     parts = np.stack([np.cos(angle) * factor, -np.sin(angle) * factor])
     parts = parts.astype(np.float32).astype(ml_dtypes.bfloat16)[:, index]
-    parts = parts.reshape(2, X, Z, 8, H, HC, N).transpose(2, 4, 0, 1, 3, 5, 6)
-    return np.ascontiguousarray(parts.reshape(Z, H, 2 * C // UNITS, N))
+    parts = parts.reshape(2, X, Z, 8, Q, QC, N).transpose(2, 4, 0, 1, 3, 5, 6)
+    return np.ascontiguousarray(parts.reshape(Z, Q, 2 * C // UNITS, N))
 
 
 def correlate(order, slot, block, store):
@@ -59,7 +60,7 @@
     p = one(4) + one(7) + one(9)
     q = entry - (3 * one(4) + 2 * one(7) + one(9))
     for i in range(I):
-        for ch in range(HC):
+        for ch in range(QC):
             left, twisted, right = [], [], []
             for g in range(G):
                 data = block(g, i, ch, p)
@@ -85,8 +86,8 @@
 
 
 def main_kernel(
-    order, v_hbm, coef_hbm, tab_hbm, early, late, v, coef, x, fs, fb, tab, sf, s, b, c, r,
-    load_sem, tab_sem, plane_send, plane_recv, send, recv,
+    order, v_hbm, coef_hbm, tab_hbm, early, late, v, coef, x, fs, fb, tab, sf, s, b, c, r0, r1, r2,
+    ring_in, plane_in, load_sem, tab_sem, plane_send, plane_recv, send, recv,
 ):
     grp = lax.axis_index("grp")
     dev = lax.axis_index("dev")
@@ -169,7 +170,7 @@
     rows = C // UNITS
     low = lax.broadcasted_iota(jnp.int32, (rows, LANES), 1) < F
 
-    def make(u, carry):
+    def make(u):
         table_copy(u).wait()
         spectra = lax.dot_general(
             tab[u], fb[...], (((1,), (1,)), ((), ())), preferred_element_type=F32
@@ -181,117 +182,163 @@
                 im = spectra[rows:, tile : tile + LANES]
                 even = jnp.where(low, re, pltpu.roll(im, F, 1))
                 odd = jnp.where(low, pltpu.roll(re, F, 1), im)
-                sf[i, pl.ds(2 * pair, rows, stride=LOCAL), :] = even
-                sf[i, pl.ds(2 * pair + 1, rows, stride=LOCAL), :] = odd
-            s[u, :, i] = sf[i].reshape(PLANE, PIECE, LANES).astype(BF16)
-
-        def spread(n, carry):
+                at = i * LOCAL + 2 * pair
+                sf[pl.ds(at, rows, stride=I * LOCAL), :] = even
+                sf[pl.ds(at + 1, rows, stride=I * LOCAL), :] = odd
+        s[u] = sf[...].reshape(PLANE, PIECE, LANES).astype(BF16)
+
+    def spread(u, source, landing):
+        def one(n, carry):
             place, device = at_plane(n)
             pltpu.make_async_remote_copy(
-                s.at[u, place], b.at[u, mine], plane_send.at[u], plane_recv.at[u], device, MESH
+                source.at[place], landing.at[mine], plane_send.at[u], plane_recv.at[u], device, MESH
             ).start()
             return carry
 
-        lax.fori_loop(1, PLANE, spread, 0)
-        b[u, mine] = s[u, mine]
-        return carry
+        lax.fori_loop(1, PLANE, one, 0)
+        landing[mine] = source[mine]
+
+    def gathered(u, landing):
+        part = landing.at[pl.ds(0, PLANE - 1)]
+        pltpu.make_async_copy(part, part, plane_recv.at[u]).wait()
+
+    def ring_copy(quarter, u, other):
+        source = c.at[u - Z] if quarter else s.at[u]
+        landing = (r0, r1, r2, late)[quarter].at[grp, :, :, :, z] if quarter else ring_in.at[:, here]
+        to = lax.rem(grp + other, G)
+        return pltpu.make_async_remote_copy(
+            source,
+            landing,
+            send.at[u, other],
+            recv.at[u, other],
+            at_ring(to * Z + (z + step_of(u)) % Z),
+            MESH,
+        )
+
+    def ring_send(quarter, u, keep):
+        ring_copy(quarter, u, 1).start()
+        pl.when(u % Z == 0)(keep)
+
+        @pl.when(u % Z != 0)
+        def _():
+            ring_copy(quarter, u, 0).start()
+
+    def ring_wait(quarter, what):
+        def one(u, carry):
+            getattr(ring_copy(quarter, u, 1), what)()
+
+            @pl.when(u % Z != 0)
+            def _():
+                getattr(ring_copy(quarter, u, 0), what)()
+
+            return carry
+
+        lax.fori_loop(quarter * Z, quarter * Z + Z, one, 0)
 
     row = lax.broadcasted_iota(jnp.int32, (256, 256), 0)
     col = lax.broadcasted_iota(jnp.int32, (256, 256), 1)
-    source = (row // 128) * 128 + ((row // 4) % 8) * 16 + ((row // 32) % 4) * 4 + row % 4
+    source = (row // 128) * 128 + ((row // 4) % 8) * 16 + ((row // 32) % 2) * 8 + ((row // 64) % 2) * 4 + row % 4
     swap = (source == col).astype(F32).astype(BF16)
 
-    halves = (r, late)
-
-    def ring_copy(half, u, other):
-        to = lax.rem(grp + other, G)
-        step = step_of(u)
-        return pltpu.make_async_remote_copy(
-            c.at[u],
-            halves[half].at[grp, :, :, :, z],
-            send.at[u, other],
-            recv.at[u, other],
-            at_ring(to * Z + (z + step) % Z),
-            MESH,
+    def interleave(block, store):
+        pieces = [block(xs).reshape(128, LANES) for xs in range(X)]
+        wide = jnp.concatenate(
+            [jnp.concatenate(pieces[:2], axis=0), jnp.concatenate(pieces[2:], axis=0)], axis=1
         )
-
-    def pass_on(half, u):
-        whole = pl.ds(0, PLANE - 1)
-        pltpu.make_async_copy(b.at[u, whole], b.at[u, whole], plane_recv.at[u]).wait()
-        for pair in range(X // 2):
-            pieces = [
-                b[u, pair * 16 : pair * 16 + 16, i].reshape(256, LANES) for i in range(I)
-            ]
-            mixed = jnp.dot(swap, jnp.concatenate(pieces, axis=1), preferred_element_type=F32)
-            for i in range(I):
-                part = mixed[:, i * LANES : (i + 1) * LANES].astype(BF16)
-                part = part.reshape(2, HC, ROWS, LANES)
-                for n in range(2):
-                    c[u, i, :, pair * 2 + n] = part[n]
-        ring_copy(half, u, 1).start()
-
-        @pl.when(u % Z == 0)
-        def _():
-            halves[half][grp, :, :, :, z] = c[u]
-
-        @pl.when(u % Z != 0)
-        def _():
-            ring_copy(half, u, 0).start()
-
-    lax.fori_loop(0, Z, make, 0)
-
-    def both(u, carry):
-        pass_on(0, u)
-        return make(u + Z, carry)
-
-    lax.fori_loop(0, Z, both, 0)
+        mixed = jnp.dot(swap, wide, preferred_element_type=F32)
+        for xs in range(X):
+            at, lane = xs % 2 * 128, xs // 2 * LANES
+            part = mixed[at : at + 128, lane : lane + LANES].astype(BF16)
+            store(xs, part.reshape(I, QC, ROWS, LANES))
+
+    def first(u, carry):
+        make(u)
+
+        def keep():
+            ring_in[:, here] = s[u]
+
+        ring_send(0, u, keep)
+        return carry
+
+    def start(u, carry):
+        make(u)
+        spread(u, s.at[u], b.at[u - Z])
+        return carry
+
+    def pass_on(quarter, u):
+        gathered(u, b.at[u - Z])
+
+        def store(xs, part):
+            c[u - Z, :, :, xs] = part
+
+        interleave(lambda xs: b[u - Z, xs * 8 : xs * 8 + 8], store)
+
+        def keep():
+            (r0, r1, r2, late)[quarter][grp, :, :, :, z] = c[u - Z]
+
+        ring_send(quarter, u, keep)
+
+    lax.fori_loop(0, Z, first, 0)
+    lax.fori_loop(Z, 2 * Z, start, 0)
+    for quarter in range(1, Q - 1):
+
+        def both(u, carry, quarter=quarter):
+            pass_on(quarter, u)
+            return start(u + Z, carry)
+
+        lax.fori_loop(quarter * Z, quarter * Z + Z, both, 0)
+
+    ring_wait(0, "wait_recv")
+    spread(0, ring_in, plane_in)
 
     def rest(u, carry):
-        pass_on(1, u)
-        return carry
-
-    lax.fori_loop(Z, UNITS, rest, 0)
-
-    def arrive(half):
-        def one(u, carry):
-            ring_copy(half, u, 1).wait_recv()
-
-            @pl.when(u % Z != 0)
-            def _():
-                ring_copy(half, u, 0).wait_recv()
-
+        pass_on(Q - 1, u)
+        return carry
+
+    lax.fori_loop(UNITS - Z, UNITS, rest, 0)
+
+    gathered(0, plane_in)
+
+    def turn(n, carry):
+        def store(xs, part):
+            r0[n // Z, :, :, xs, n % Z] = part
+
+        interleave(lambda xs: plane_in[xs * 8 : xs * 8 + 8, n], store)
+        return carry
+
+    lax.fori_loop(0, G * Z, turn, 0)
+
+    def sums(quarter, r):
+        def one(n, carry):
+            def block(g, i, ch, p):
+                return r[g, i, ch, p].reshape(LANES, LANES)
+
+            def store(i, ch, re, im):
+                early[n, i, 0, quarter * QC + ch] = re
+                early[n, i, 1, quarter * QC + ch] = im
+
+            correlate(order, grp * SLOTS + n, block, store)
             return carry
 
-        lax.fori_loop(half * Z, half * Z + Z, one, 0)
-
-    arrive(0)
-
-    def early_slot(n, carry):
-        def block(g, i, ch, p):
-            return r[g, i, ch, p].reshape(LANES, LANES)
-
-        def store(i, ch, re, im):
-            early[n, i, 0, ch] = re
-            early[n, i, 1, ch] = im
-
-        correlate(order, grp * SLOTS + n, block, store)
-        return carry
-
-    lax.fori_loop(0, SLOTS, early_slot, 0)
-    arrive(1)
+        lax.fori_loop(0, SLOTS, one, 0)
+
+    sums(0, r0)
+    ring_wait(1, "wait_recv")
+    sums(1, r1)
+    ring_wait(2, "wait_recv")
+    sums(2, r2)
+    for quarter in range(Q):
+        ring_wait(quarter, "wait_send")
+    part = ring_in.at[pl.ds(0, PLANE - 1)]
+    pltpu.make_async_copy(part, part, plane_send.at[0]).wait()
 
     def sent(u, carry):
-        ring_copy(0, u, 1).wait_send()
-
-        @pl.when(u % Z != 0)
-        def _():
-            ring_copy(0, u, 0).wait_send()
-
-        whole = pl.ds(0, PLANE - 1)
-        pltpu.make_async_copy(s.at[u, whole], s.at[u, whole], plane_send.at[u]).wait()
-        return carry
-
-    lax.fori_loop(0, UNITS, sent, 0)
+        part = s.at[u, pl.ds(0, PLANE - 1)]
+        pltpu.make_async_copy(part, part, plane_send.at[u]).wait()
+        return carry
+
+    lax.fori_loop(Z, UNITS, sent, 0)
+    ring_wait(Q - 1, "wait_recv")
 
 
 def main(block_order, voltages):
@@ -302,8 +349,8 @@
         main_kernel,
         name="main",
         out_shape=(
-            pltpu.VMEM((SLOTS, I, 2, HC, LANES, LANES), F32),
-            pltpu.VMEM((G, I, HC, X, Z, ROWS, LANES), BF16),
+            pltpu.VMEM((SLOTS, I, 2, EARLY, LANES, LANES), F32),
+            pltpu.VMEM((G, I, QC, X, Z, ROWS, LANES), BF16),
         ),
         in_specs=[pl.BlockSpec(memory_space=pltpu.SMEM), hbm, hbm, hbm],
         out_specs=(pl.BlockSpec(memory_space=pltpu.VMEM), pl.BlockSpec(memory_space=pltpu.VMEM)),
@@ -314,11 +361,15 @@
             pltpu.VMEM((I * LOCAL * STEP, LANES), F32),
             pltpu.VMEM((I * LOCAL * F, N), BF16),
             pltpu.VMEM((UNITS, 2 * C // UNITS, N), BF16),
-            pltpu.VMEM((I, C // UNITS * LOCAL, LANES), F32),
-            pltpu.VMEM((UNITS, PLANE, I, PIECE, LANES), BF16),
-            pltpu.VMEM((UNITS, PLANE, I, PIECE, LANES), BF16),
-            pltpu.VMEM((UNITS, I, HC, X, ROWS, LANES), BF16),
-            pltpu.VMEM((G, I, HC, X, Z, ROWS, LANES), BF16),
+            pltpu.VMEM((C // UNITS * I * LOCAL, LANES), F32),
+            pltpu.VMEM((UNITS, PLANE, PIECE, LANES), BF16),
+            pltpu.VMEM((UNITS - Z, PLANE, PIECE, LANES), BF16),
+            pltpu.VMEM((UNITS - Z, I, QC, X, ROWS, LANES), BF16),
+            pltpu.VMEM((G, I, QC, X, Z, ROWS, LANES), BF16),
+            pltpu.VMEM((G, I, QC, X, Z, ROWS, LANES), BF16),
+            pltpu.VMEM((G, I, QC, X, Z, ROWS, LANES), BF16),
+            pltpu.VMEM((PLANE, G * Z, PIECE, LANES), BF16),
+            pltpu.VMEM((PLANE, G * Z, PIECE, LANES), BF16),
             pltpu.SemaphoreType.DMA((1 + SPLIT * I,)),
             pltpu.SemaphoreType.DMA((UNITS,)),
             pltpu.SemaphoreType.DMA((UNITS,)),
@@ -333,12 +384,12 @@
 
 
 def last_kernel(order, early, late, out, results, early_sem, sems):
-    first = pltpu.make_async_copy(early, out.at[:, :, :, pl.ds(0, HC)], early_sem)
+    first = pltpu.make_async_copy(early, out.at[:, :, :, pl.ds(0, EARLY)], early_sem)
     first.start()
     grp = lax.axis_index("grp")
 
     def result(n):
-        return pltpu.make_async_copy(results.at[n], out.at[n, :, :, pl.ds(HC, HC)], sems.at[n])
+        return pltpu.make_async_copy(results.at[n], out.at[n, :, :, pl.ds(EARLY, QC)], sems.at[n])
 
     def slot(n, carry):
         def block(g, i, ch, p):
@@ -367,7 +418,7 @@
         in_specs=[pl.BlockSpec(memory_space=pltpu.SMEM), vmem, vmem],
         out_specs=pl.BlockSpec(memory_space=pltpu.HBM),
         scratch_shapes=[
-            pltpu.VMEM((SLOTS, I, 2, HC, LANES, LANES), F32),
+            pltpu.VMEM((SLOTS, I, 2, QC, LANES, LANES), F32),
             pltpu.SemaphoreType.DMA,
             pltpu.SemaphoreType.DMA((SLOTS,)),
         ],

time: 120 us -> 112 us (0.933)
  Pallas kernels: 120 us -> 112 us
    pallas_call x1, Pallas kernels: 116 us -> 107 us  [main(): pl.pallas_call(main_kernel, name='main', out_shape=(pltpu.VMEM((SLOTS, I,...]
where the time goes in v3:
time: 112 us
  Pallas kernels  112 us (100%)
    pallas_call x1, Pallas kernels, main(): pl.pallas_call(main_kernel, name='main', out_shape=(pltpu.VMEM((SLOTS, I,...  107 us
    pallas_call x1, Pallas kernels, last(): pl.pallas_call(last_kernel, name='last', out_shape=jax.ShapeDtypeStruct((...  4.6 us

profile of v3, /device:TPU:1, one launch (start us, length us, event | category | flops | bytes accessed | tf_op | source)
XLA Modules:
  0.0 112.0 jit_solution(14828281499598023143)
XLA Ops:
  0.0 0.0 copy-start
  0.0 107.4 %main.1 = (f32[5,2,2,6,128,128]{5,4,3,2,1,0:T(8,128)S(1)}, bf16[2,2,2,4,4,32,128]{6,5,4,3,2,1,0:T(8,128)(2,1)S(1)}) custom-call(s32[10]{0:T(128)} %order.3, s32[4,68608]{1,0:T(4,128)} %v_hbm.1, f32[64,128]{1,0:T(8,128)} %constant.4.clone.coef_hbm, bf16[4,4,128,2048]{3,2,1,0:T(8,128)(2,1)} %constant.5.clone.tab_hbm), custom_call_target="tpu_custom_call" | custom-call | tf_op jit(solution)/shard_map/main/pallas_call | solution.py:348
  107.4 0.0 copy-done
  107.4 4.6 %last.1 = f32[5,2,2,8,128,128]{5,4,3,2,1,0:T(8,128)} custom-call(s32[10]{0:T(128)S(1)} %copy-done, f32[5,2,2,6,128,128]{5,4,3,2,1,0:T(8,128)S(1)} %get-tuple-element.7.early, bf16[2,2,2,4,4,32,128]{6,5,4,3,2,1,0:T(8,128)(2,1)S(1)} %get-tuple-element.8.late), custom_call_target="tpu_custom_call" | custom-call | tf_op jit(solution)/shard_map/last/pallas_call | solution.py:414
Async XLA Ops:
  0.0 107.4 %copy-start = (s32[10]{0:T(128)S(1)}, s32[10]{0:T(128)}, u32[]{:S(2)}) copy-start(s32[10]{0:T(128)} %order.3) | copy-start | bytes 124

commit v4 on v3

--- a/solution.py
+++ b/solution.py
@@ -30,8 +30,7 @@
 EARLY = (Q - 1) * QC
 ROWS = 8 * LOCAL
 UNITS = Q * Z
-STEP = F + 8
-SPLIT = 2
+SPLIT = 4
 WORDS = 34304
 TILES = WORDS // LANES
 SLOTS = 5
@@ -82,12 +81,13 @@
 
 
 def step_of(u):
-    return 2 * ((u % Z) % 2) + (u % Z) // 2
+    n = u % Z
+    return n + n // 2 - 2 * (n // 3)
 
 
 def main_kernel(
-    order, v_hbm, coef_hbm, tab_hbm, early, late, v, coef, x, fs, fb, tab, sf, s, b, c, r0, r1, r2,
-    ring_in, plane_in, load_sem, tab_sem, plane_send, plane_recv, send, recv,
+    order_hbm, v_hbm, coef_hbm, tab_hbm, early, late, order, v, coef, x, fb, regroup, total, tab, sf, s, b, c, r0, r1, r2,
+    ring_in, plane_in, order_sem, load_sem, tab_sem, plane_send, plane_recv, send, recv,
 ):
     grp = lax.axis_index("grp")
     dev = lax.axis_index("dev")
@@ -102,6 +102,10 @@
     def at_ring(height):
         height = lax.rem(height, G * Z)
         return (height // Z, (dev // 32) * 32 + (height % Z) * 8 + dev % 8)
+
+    def table_copy(u):
+        t = (z + step_of(u)) % Z
+        return pltpu.make_async_copy(tab_hbm.at[t, u // Z], tab.at[u], tab_sem.at[u])
 
     width = WORDS // SPLIT
     loads = [pltpu.make_async_copy(coef_hbm, coef, load_sem.at[0])]
@@ -112,6 +116,9 @@
             loads.append(pltpu.make_async_copy(v_hbm.at[:, span], v.at[:, span], load_sem.at[n]))
     for load in loads:
         load.start()
+    table_copy(0).start()
+    slots = pltpu.make_async_copy(order_hbm, order, order_sem)
+    slots.start()
 
     barrier = pltpu.get_barrier_semaphore()
 
@@ -126,6 +133,10 @@
 
     lax.fori_loop(1, PLANE, greet_plane, 0)
     lax.fori_loop(1, G * Z, greet_ring, 0)
+
+    row = lax.broadcasted_iota(jnp.int32, regroup.shape, 0)
+    col = lax.broadcasted_iota(jnp.int32, regroup.shape, 1)
+    regroup[...] = ((col % F) * (I * LOCAL) + col // F == row).astype(F32).astype(BF16)
 
     def unpack(tile, carry):
         at = pl.multiple_of(tile * LANES, LANES)
@@ -135,36 +146,53 @@
             x[byte * TILES + tile] = raw.astype(F32)
         return carry
 
-    def table_copy(u):
-        t = (z + step_of(u)) % Z
-        return pltpu.make_async_copy(tab_hbm.at[t, u // Z], tab.at[u], tab_sem.at[u])
-
     for part in range(SPLIT):
         for i in range(I):
             loads[1 + part * I + i].wait()
         if part == SPLIT - 1:
-            for u in range(UNITS):
+            for u in range(1, UNITS):
                 table_copy(u).start()
         tiles = TILES // SPLIT
         lax.fori_loop(part * tiles, (part + 1) * tiles, unpack, 0, unroll=2)
     loads[0].wait()
 
-    def fir(nb, carry):
+    def fir(nb):
         taps = [coef[pl.ds(nb * TAPS + k, 1), :] for k in range(TAPS)]
         window = [x[k * NB + nb] for k in range(TAPS - 1)]
-        for f in range(F):
-            window.append(x[(f + TAPS - 1) * NB + nb])
-            total = window[0] * taps[0]
-            for k in range(1, TAPS):
-                total = total + window[k] * taps[k]
-            window.pop(0)
-            fs[pl.ds(f, 8, stride=STEP), :] = total
         at = pl.ds(pl.multiple_of(nb * LANES, LANES), LANES)
-        for row in range(I * LOCAL):
-            fb[row * F : (row + 1) * F, at] = fs[row * STEP : row * STEP + F, :].astype(BF16)
-        return carry
-
-    lax.fori_loop(0, NB, fir, 0)
+        for f in range(0, F, 2):
+            sums = []
+            for n in range(2):
+                window.append(x[(f + n + TAPS - 1) * NB + nb])
+                one = window[0] * taps[0]
+                for k in range(1, TAPS):
+                    one = one + window[k] * taps[k]
+                window.pop(0)
+                sums.append(one)
+            fb[f * 8 : f * 8 + 16, at] = jnp.concatenate(sums, axis=0).astype(BF16)
+
+    def dft(table, frames):
+        return lax.dot_general(
+            table, frames, (((1,), (1,)), ((), ())), preferred_element_type=F32
+        )
+
+    def partial(n):
+        at = pl.ds(pl.multiple_of(n * 2 * LANES, 2 * LANES), 2 * LANES)
+        return dft(tab[0, :, at], fb[:, at])
+
+    fir(0)
+    fir(1)
+    table_copy(0).wait()
+    total[...] = jnp.zeros_like(total)
+
+    def blocks(n, carry):
+        total[...] += partial(n - 1)
+        fir(2 * n)
+        fir(2 * n + 1)
+        return carry
+
+    lax.fori_loop(1, NB // 2, blocks, 0)
+    total[...] += partial(NB // 2 - 1)
     pl.semaphore_wait(barrier, PLANE + G * Z - 2)
 
     rows = C // UNITS
@@ -172,9 +200,10 @@
 
     def make(u):
         table_copy(u).wait()
-        spectra = lax.dot_general(
-            tab[u], fb[...], (((1,), (1,)), ((), ())), preferred_element_type=F32
-        )
+        finish(u, dft(tab[u], fb[...]))
+
+    def finish(u, spectra):
+        spectra = jnp.dot(spectra.astype(BF16), regroup[...], preferred_element_type=F32)
         for i in range(I):
             for pair in range(LOCAL // 2):
                 tile = (i * LOCAL // 2 + pair) * LANES
@@ -251,13 +280,15 @@
             part = mixed[at : at + 128, lane : lane + LANES].astype(BF16)
             store(xs, part.reshape(I, QC, ROWS, LANES))
 
+    def ring_first(u):
+        def keep():
+            ring_in[:, here] = s[u]
+
+        ring_send(0, u, keep)
+
     def first(u, carry):
         make(u)
-
-        def keep():
-            ring_in[:, here] = s[u]
-
-        ring_send(0, u, keep)
+        ring_first(u)
         return carry
 
     def start(u, carry):
@@ -278,7 +309,9 @@
 
         ring_send(quarter, u, keep)
 
-    lax.fori_loop(0, Z, first, 0)
+    finish(0, total[...])
+    ring_first(0)
+    lax.fori_loop(1, Z, first, 0)
     lax.fori_loop(Z, 2 * Z, start, 0)
     for quarter in range(1, Q - 1):
 
@@ -322,6 +355,7 @@
 
         lax.fori_loop(0, SLOTS, one, 0)
 
+    slots.wait()
     sums(0, r0)
     ring_wait(1, "wait_recv")
     sums(1, r1)
@@ -352,14 +386,16 @@
             pltpu.VMEM((SLOTS, I, 2, EARLY, LANES, LANES), F32),
             pltpu.VMEM((G, I, QC, X, Z, ROWS, LANES), BF16),
         ),
-        in_specs=[pl.BlockSpec(memory_space=pltpu.SMEM), hbm, hbm, hbm],
+        in_specs=[hbm, hbm, hbm, hbm],
         out_specs=(pl.BlockSpec(memory_space=pltpu.VMEM), pl.BlockSpec(memory_space=pltpu.VMEM)),
         scratch_shapes=[
+            pltpu.SMEM((10,), jnp.int32),
             pltpu.VMEM((LOCAL, I * WORDS), jnp.int32),
             pltpu.VMEM((NB * TAPS, LANES), F32),
             pltpu.VMEM((4 * TILES, I * LOCAL, LANES), F32),
-            pltpu.VMEM((I * LOCAL * STEP, LANES), F32),
             pltpu.VMEM((I * LOCAL * F, N), BF16),
+            pltpu.VMEM((I * LOCAL * F, I * LOCAL * F), BF16),
+            pltpu.VMEM((2 * C // UNITS, I * LOCAL * F), F32),
             pltpu.VMEM((UNITS, 2 * C // UNITS, N), BF16),
             pltpu.VMEM((C // UNITS * I * LOCAL, LANES), F32),
             pltpu.VMEM((UNITS, PLANE, PIECE, LANES), BF16),
@@ -370,6 +406,7 @@
             pltpu.VMEM((G, I, QC, X, Z, ROWS, LANES), BF16),
             pltpu.VMEM((PLANE, G * Z, PIECE, LANES), BF16),
             pltpu.VMEM((PLANE, G * Z, PIECE, LANES), BF16),
+            pltpu.SemaphoreType.DMA,
             pltpu.SemaphoreType.DMA((1 + SPLIT * I,)),
             pltpu.SemaphoreType.DMA((UNITS,)),
             pltpu.SemaphoreType.DMA((UNITS,)),
@@ -383,7 +420,9 @@
     )(block_order, voltages, coef, table)
 
 
-def last_kernel(order, early, late, out, results, early_sem, sems):
+def last_kernel(order_hbm, early, late, out, order, results, order_sem, early_sem, sems):
+    slots = pltpu.make_async_copy(order_hbm, order, order_sem)
+    slots.start()
     first = pltpu.make_async_copy(early, out.at[:, :, :, pl.ds(0, EARLY)], early_sem)
     first.start()
     grp = lax.axis_index("grp")
@@ -403,6 +442,7 @@
         result(n).start()
         return carry
 
+    slots.wait()
     lax.fori_loop(0, SLOTS, slot, 0)
     first.wait()
     for n in range(SLOTS):
@@ -415,10 +455,12 @@
         last_kernel,
         name="last",
         out_shape=jax.ShapeDtypeStruct((SLOTS, I, 2, CH, LANES, LANES), F32),
-        in_specs=[pl.BlockSpec(memory_space=pltpu.SMEM), vmem, vmem],
+        in_specs=[pl.BlockSpec(memory_space=pltpu.HBM), vmem, vmem],
         out_specs=pl.BlockSpec(memory_space=pltpu.HBM),
         scratch_shapes=[
+            pltpu.SMEM((10,), jnp.int32),
             pltpu.VMEM((SLOTS, I, 2, QC, LANES, LANES), F32),
+            pltpu.SemaphoreType.DMA,
             pltpu.SemaphoreType.DMA,
             pltpu.SemaphoreType.DMA((SLOTS,)),
         ],

time: 112 us -> 109 us (0.973)
  Pallas kernels: 112 us -> 109 us
    pallas_call x1, Pallas kernels: 107 us -> 105 us  [main(): pl.pallas_call(main_kernel, name='main', out_shape=(pltpu.VMEM((SLOTS, I,...]
where the time goes in v4:
time: 109 us
  Pallas kernels  109 us (100%)
    pallas_call x1, Pallas kernels, main(): pl.pallas_call(main_kernel, name='main', out_shape=(pltpu.VMEM((SLOTS, I,...  105 us
    pallas_call x1, Pallas kernels, last(): pl.pallas_call(last_kernel, name='last', out_shape=jax.ShapeDtypeStruct((...  4.07 us

profile of v4, /device:TPU:1, one launch (start us, length us, event | category | flops | bytes accessed | tf_op | source)
XLA Modules:
  0.0 108.7 jit_solution(2760000847698605664)
XLA Ops:
  0.0 0.0 copy-start
  0.0 104.6 %main.1 = (f32[5,2,2,6,128,128]{5,4,3,2,1,0:T(8,128)S(1)}, bf16[2,2,2,4,4,32,128]{6,5,4,3,2,1,0:T(8,128)(2,1)S(1)}) custom-call(s32[10]{0:T(128)} %order_hbm.3, s32[4,68608]{1,0:T(4,128)} %v_hbm.1, f32[64,128]{1,0:T(8,128)} %constant.4.clone.coef_hbm, bf16[4,4,128,2048]{3,2,1,0:T(8,128)(2,1)} %constant.5.clone.tab_hbm), custom_call_target="tpu_custom_call" | custom-call | tf_op jit(solution)/shard_map/main/pallas_call | solution.py:382
  104.6 0.0 copy-done
  104.6 4.1 %last.1 = f32[5,2,2,8,128,128]{5,4,3,2,1,0:T(8,128)} custom-call(s32[10]{0:T(128)S(1)} %copy-done, f32[5,2,2,6,128,128]{5,4,3,2,1,0:T(8,128)S(1)} %get-tuple-element.7.early, bf16[2,2,2,4,4,32,128]{6,5,4,3,2,1,0:T(8,128)(2,1)S(1)} %get-tuple-element.8.late), custom_call_target="tpu_custom_call" | custom-call | tf_op jit(solution)/shard_map/last/pallas_call | solution.py:454
Async XLA Ops:
  0.0 104.6 %copy-start = (s32[10]{0:T(128)S(1)}, s32[10]{0:T(128)}, u32[]{:S(2)}) copy-start(s32[10]{0:T(128)} %order_hbm.3) | copy-start | bytes 124
